TPU v7x, 16 devices: a whole 2x2x2 slice. The times are simulated.
16 devices in a mesh: dp: 2 (over z), tp: 8 (over y, x, core).
Axes of the slice: x: 2, y: 2, z: 2, core: 2. Of those that a mesh axis runs over, the one named last changes fastest.
Arguments:
- hidden_in: bfloat16 [64, 2048], P('dp'), parts along dimension 0
- k_cache: bfloat16 [64, 256, 16, 128], P('dp', None, 'tp'), parts along dimension 0
- v_cache: bfloat16 [64, 256, 16, 128], P('dp', None, 'tp'), parts along dimension 0
- seq_lens: int32 [64], P('dp'), parts along dimension 0
- chosen_experts: int32 [64, 6], P('dp'), parts along dimension 0
- g_attn: bfloat16 [2048], replicated
- w_q: bfloat16 [2048, 2048], P(None, 'tp')
- w_k: bfloat16 [2048, 2048], P(None, 'tp')
- w_v: bfloat16 [2048, 2048], P(None, 'tp')
- w_o: bfloat16 [2048, 2048], P('tp')
- g_moe: bfloat16 [2048], replicated
- w_router: bfloat16 [2048, 64], replicated
- w_gate: bfloat16 [64, 2048, 1408], P(None, None, 'tp')
- w_up: bfloat16 [64, 2048, 1408], P(None, None, 'tp')
- w_down: bfloat16 [64, 1408, 2048], P(None, 'tp')
Outputs:
- output 1: bfloat16 [64, 2048], P('dp'), parts along dimension 0
- output 2: bfloat16 [64, 256, 16, 128], P('dp', None, 'tp'), parts along dimension 0
- output 3: bfloat16 [64, 256, 16, 128], P('dp', None, 'tp'), parts along dimension 0
There are 2 independent parts. A program takes and returns all parts, laid end to end along the dimension named above; an argument that names none is the same for every part.
All inputs are finite; a program needn't handle non-finite values.
Results may differ from a plain program's by a relative error of at most 0.0145238.
Values are sent between devices in bfloat16 or wider.
A program may use at most 1 GiB of HBM per device.

v0:
```python
import functools

import jax
import jax.numpy as jnp
import numpy as np
from jax import lax
from jax.experimental import pallas as pl
from jax.experimental.pallas import tpu as pltpu
from jax.sharding import PartitionSpec as P

EPSILON = 1e-5
ROPE_THETA = 1000000.0
MASK_FILL = -1e30
F32 = jnp.float32
BF16 = jnp.bfloat16
ANY = pl.BlockSpec(memory_space=pltpu.HBM)
VMEM = pl.BlockSpec(memory_space=pltpu.VMEM)
SMEM = pl.BlockSpec(memory_space=pltpu.SMEM)
NT = (((1,), (1,)), ((), ()))

GROUP = 8
RING = 8
HELD = 12


def norm_rows(x, gain):
    x32 = x.astype(F32)
    scale = lax.rsqrt(jnp.mean(x32 * x32, axis=-1, keepdims=True) + EPSILON)
    gain32 = gain.astype(F32)
    gain_row = jnp.concatenate([gain32[i:i + 1, :] for i in range(gain.shape[0])], axis=1)
    return (x32 * scale * gain_row).astype(BF16)


def attention_kernel(x_ref, lens_ref, chosen_ref, gain_ref, freq_ref, wq_hbm, wk_hbm, wv_hbm, wo_hbm, k_hbm, v_hbm,
                     part_ref, list_ref, ko_hbm, vo_hbm,
                     wq, wk, wv, wo, kbuf, vbuf, qs, ks, vs, os, wsem, ksem, vsem, kosem, vosem):
    rows, width = x_ref.shape
    slots2, dim = kbuf.shape[1], kbuf.shape[2]
    steps = rows // GROUP

    def load(hbm, buf, sem):
        return pltpu.make_async_copy(hbm, buf, sem)

    def part(hbm, buf, sem, c):
        block = pl.ds(c * GROUP, GROUP)
        return pltpu.make_async_copy(hbm.at[block], buf.at[block], sem.at[c])

    weights = [load(wq_hbm, wq, wsem.at[0]), load(wk_hbm, wk, wsem.at[1]), load(wv_hbm, wv, wsem.at[2]), load(wo_hbm, wo, wsem.at[3])]
    for copy in weights[:3]:
        copy.start()
    for c in range(steps):
        part(k_hbm, kbuf, ksem, c).start()
        part(v_hbm, vbuf, vsem, c).start()
    weights[3].start()

    experts = 64
    sub = lax.broadcasted_iota(jnp.int32, (experts, rows), 0)
    hit = chosen_ref[0:1, :] == sub
    for k in range(1, chosen_ref.shape[0]):
        hit = hit | (chosen_ref[k:k + 1, :] == sub)
    used_col = jnp.max(hit.astype(F32), axis=1, keepdims=True)
    si = lax.broadcasted_iota(jnp.int32, (experts, 128), 0)
    li = lax.broadcasted_iota(jnp.int32, (experts, 128), 1)
    used_row = jnp.sum(jnp.where(si == li, used_col, 0.0), axis=0, keepdims=True)
    rank_col = jnp.sum(jnp.where(li < si, used_row, 0.0), axis=1, keepdims=True)
    pick = (rank_col == li.astype(F32)) & (used_col > 0.0)
    ids = jnp.sum(jnp.where(pick, si.astype(F32), 0.0), axis=0, keepdims=True)
    total = jnp.sum(used_row, axis=1, keepdims=True)
    lane1 = lax.broadcasted_iota(jnp.int32, (1, 128), 1)
    held = jnp.sum(jnp.where(lane1 < HELD, used_row, 0.0), axis=1, keepdims=True)
    list_ref[...] = jnp.where(lane1 == 127, total, jnp.where(lane1 == 126, held, ids)).astype(jnp.int32)

    h = norm_rows(x_ref[...], gain_ref[...])

    row_id = lax.broadcasted_iota(jnp.int32, (rows, dim), 0)
    pos = jnp.zeros((rows, dim), F32)
    for b in range(rows):
        pos = jnp.where(row_id == b, lens_ref[b].astype(F32), pos)
    angle = pos * freq_ref[...]
    cos_t = jnp.cos(angle)
    lane = lax.broadcasted_iota(jnp.int32, (rows, dim), 1)
    sin_t = jnp.where(lane < dim // 2, -jnp.sin(angle), jnp.sin(angle))

    def rope(y):
        return y * cos_t + pltpu.roll(y, dim // 2, 1) * sin_t

    def project(copy, w):
        copy.wait()
        return jnp.dot(h, w[...], preferred_element_type=F32)

    q = project(weights[0], wq)
    k = project(weights[1], wk)
    v = project(weights[2], wv)
    for j in range(2):
        cols = slice(j * dim, (j + 1) * dim)
        qs[:, cols] = rope(q[:, cols]).astype(BF16).astype(F32)
        ks[:, cols] = rope(k[:, cols]).astype(BF16).astype(F32)
        vs[:, cols] = v[:, cols].astype(BF16).astype(F32)

    r16 = lax.broadcasted_iota(jnp.int32, (16, dim), 0)
    srow = lax.broadcasted_iota(jnp.int32, (16, slots2), 0)
    scol = lax.broadcasted_iota(jnp.int32, (16, slots2), 1)
    same_head = (srow % 2) == (scol % 2)
    slot = scol // 2

    def put_row(buf, new, b, p):
        tile = pl.ds(pl.multiple_of((p // 8) * 16, 16), 16)
        old = buf[b, tile, :].astype(F32)
        head = jnp.where(r16 % 2 == 0, new[pl.ds(b, 1), 0:dim], new[pl.ds(b, 1), dim:2 * dim])
        buf[b, tile, :] = jnp.where(r16 // 2 == p % 8, head, old).astype(BF16)

    for c in range(steps):
        part(k_hbm, kbuf, ksem, c).wait()
        part(v_hbm, vbuf, vsem, c).wait()
        qblocks = []
        limit = jnp.zeros((16, slots2), jnp.int32)
        for j in range(GROUP):
            b = c * GROUP + j
            p = lens_ref[b]
            put_row(kbuf, ks, b, p)
            put_row(vbuf, vs, b, p)
            limit = jnp.where(srow // 2 == j, p, limit)
            qblocks.append(jnp.where(r16 == 2 * j, qs[b:b + 1, 0:dim], jnp.where(r16 == 2 * j + 1, qs[b:b + 1, dim:2 * dim], 0.0)))
        score = jnp.zeros((16, slots2), F32)
        for j in range(0, GROUP, 2):
            b = c * GROUP + j
            lhs = jnp.concatenate([qblocks[j], qblocks[j + 1]], axis=1).astype(BF16)
            rhs = jnp.concatenate([kbuf[b], kbuf[b + 1]], axis=1)
            score = score + lax.dot_general(lhs, rhs, NT, preferred_element_type=F32)
        score = score * (dim ** -0.5)
        valid = same_head & (slot <= limit)
        score = jnp.where(valid, score, MASK_FILL)
        top = jnp.max(score, axis=1, keepdims=True)
        e = jnp.where(valid, jnp.exp(score - top), 0.0)
        w = (e / jnp.sum(e, axis=1, keepdims=True)).astype(BF16)
        out = jnp.zeros((16, dim), F32)
        for j in range(0, GROUP, 2):
            b = c * GROUP + j
            rhs = jnp.concatenate([vbuf[b], vbuf[b + 1]], axis=1)
            both = jnp.dot(w, rhs, preferred_element_type=F32)
            out = jnp.where(r16 // 2 == j, both[:, 0:dim], out)
            out = jnp.where(r16 // 2 == j + 1, both[:, dim:2 * dim], out)
        os[c * 16:(c + 1) * 16, :] = out
        part(kbuf, ko_hbm, kosem, c).start()
        part(vbuf, vo_hbm, vosem, c).start()

    heads = jnp.concatenate([os[pl.ds(0, rows, stride=2), :], os[pl.ds(1, rows, stride=2), :]], axis=1).astype(BF16)
    weights[3].wait()
    for j in range(0, width, 256):
        part_ref[:, j:j + 256] = jnp.dot(heads, wo[:, j:j + 256], preferred_element_type=F32)
    for c in range(steps):
        part(kbuf, ko_hbm, kosem, c).wait()
        part(vbuf, vo_hbm, vosem, c).wait()


def attention(x, lens, chosen_t, gain, freq, wq, wk, wv, wo, k_cache, v_cache):
    rows, width = x.shape
    steps = rows // GROUP
    return pl.pallas_call(
        attention_kernel,
        name="attention",
        out_shape=(
            jax.ShapeDtypeStruct((rows, width), F32),
            jax.ShapeDtypeStruct((1, 128), jnp.int32),
            jax.ShapeDtypeStruct(k_cache.shape, BF16),
            jax.ShapeDtypeStruct(v_cache.shape, BF16),
        ),
        in_specs=[VMEM, SMEM, VMEM, VMEM, VMEM] + [ANY] * 6,
        out_specs=(VMEM, VMEM, ANY, ANY),
        scratch_shapes=[
            pltpu.VMEM(wq.shape, BF16), pltpu.VMEM(wk.shape, BF16), pltpu.VMEM(wv.shape, BF16), pltpu.VMEM(wo.shape, BF16),
            pltpu.VMEM(k_cache.shape, BF16), pltpu.VMEM(v_cache.shape, BF16),
            pltpu.VMEM((rows, 256), F32), pltpu.VMEM((rows, 256), F32), pltpu.VMEM((rows, 256), F32),
            pltpu.VMEM((2 * rows, 128), F32),
            pltpu.SemaphoreType.DMA((4,)),
            pltpu.SemaphoreType.DMA((steps,)), pltpu.SemaphoreType.DMA((steps,)),
            pltpu.SemaphoreType.DMA((steps,)), pltpu.SemaphoreType.DMA((steps,)),
        ],
        compiler_params=pltpu.CompilerParams(vmem_limit_bytes=62 * 1024 * 1024),
    )(x, lens, chosen_t, gain, freq, wq, wk, wv, wo, k_cache, v_cache)


def sum_kernel(n, n_ahead, part_ref, base_ref, *refs):
    ahead_hbm, (out_ref, *ahead), (inbox, piece, send1, recv1, send2, recv2, *sems) = (
        refs[:n_ahead], refs[n_ahead:2 * n_ahead + 1], refs[2 * n_ahead + 1:])
    me = lax.axis_index("tp")
    loads = [pltpu.make_async_copy(src.at[pl.ds(e, 2)], dst.at[pl.ds(e, 2)], sems[0].at[m, e // 2])
             for e in range(0, HELD, 2) for m, (src, dst) in enumerate(zip(ahead_hbm, ahead))]
    for load in loads:
        load.start()
    cols = part_ref.shape[1] // n
    barrier = pltpu.get_barrier_semaphore()
    for d in range(1, n):
        pl.semaphore_signal(barrier, inc=1, device_id={"tp": lax.rem(me + d, n)}, device_id_type=pl.DeviceIdType.MESH)
    pl.semaphore_wait(barrier, n - 1)

    def columns(j):
        return pl.ds(pl.multiple_of(j * cols, cols), cols)

    first = []
    for d in range(1, n):
        to = lax.rem(me + d, n)
        copy = pltpu.make_async_remote_copy(
            src_ref=part_ref.at[:, columns(to)], dst_ref=inbox.at[d - 1],
            send_sem=send1.at[d - 1], recv_sem=recv1.at[d - 1],
            device_id={"tp": to}, device_id_type=pl.DeviceIdType.MESH)
        copy.start()
        first.append(copy)
    total = part_ref[:, columns(me)]
    for d in range(1, n):
        first[d - 1].wait_recv()
        total = total + inbox[d - 1]
    piece[...] = (base_ref[:, columns(me)].astype(F32) + total).astype(BF16)
    second = []
    for d in range(1, n):
        to = lax.rem(me + d, n)
        copy = pltpu.make_async_remote_copy(
            src_ref=piece, dst_ref=out_ref.at[:, columns(me)],
            send_sem=send2.at[d - 1], recv_sem=recv2.at[d - 1],
            device_id={"tp": to}, device_id_type=pl.DeviceIdType.MESH)
        copy.start()
        second.append(copy)
    out_ref[:, columns(me)] = piece[...]
    for d in range(1, n):
        first[d - 1].wait_send()
    for d in range(1, n):
        second[d - 1].wait()
    for load in loads:
        load.wait()


def add_sum(part, base, n, collective_id, ahead=()):
    rows, width = base.shape
    return pl.pallas_call(
        functools.partial(sum_kernel, n, len(ahead)),
        name="add_sum",
        out_shape=[jax.ShapeDtypeStruct(base.shape, BF16)] + [pltpu.VMEM((HELD, *a.shape[1:]), a.dtype) for a in ahead],
        in_specs=[VMEM, VMEM] + [ANY] * len(ahead),
        out_specs=[VMEM] * (1 + len(ahead)),
        scratch_shapes=[
            pltpu.VMEM((n - 1, rows, width // n), F32), pltpu.VMEM((rows, width // n), BF16),
            pltpu.SemaphoreType.DMA((n - 1,)), pltpu.SemaphoreType.DMA((n - 1,)),
            pltpu.SemaphoreType.DMA((n - 1,)), pltpu.SemaphoreType.DMA((n - 1,)),
        ] + ([pltpu.SemaphoreType.DMA((len(ahead), HELD // 2))] if ahead else []),
        compiler_params=pltpu.CompilerParams(collective_id=collective_id, has_side_effects=True, vmem_limit_bytes=8 * 1024 * 1024),
    )(part, base, *ahead)


def experts_kernel(list_ref, x_ref, chosen_ref, gain_ref, wr_ref, held_g, held_u, held_d, gate_hbm, up_hbm, down_hbm, out_ref,
                   gates, h_ref, g_ref, u_ref, ring_g, ring_u, ring_d, sem):
    rows, width = x_ref.shape
    held, count = list_ref[0, 126], list_ref[0, 127]
    rest = count - held

    def fetch(i, go):
        slot = lax.rem(i, RING)
        e = list_ref[0, held + i]
        for m, (hbm, ring) in enumerate(((gate_hbm, ring_g), (up_hbm, ring_u), (down_hbm, ring_d))):
            copy = pltpu.make_async_copy(hbm.at[e], ring.at[slot], sem.at[m, slot])
            if go:
                copy.start()
            else:
                copy.wait()

    for i in range(RING - 2):
        @pl.when(i < rest)
        def _():
            fetch(i, True)

    h = norm_rows(x_ref[...], gain_ref[...])
    h_ref[...] = h
    logits = lax.dot_general(wr_ref[...], h, NT, preferred_element_type=F32)
    experts = logits.shape[0]
    sub = lax.broadcasted_iota(jnp.int32, (experts, rows), 0)
    hit = chosen_ref[0:1, :] == sub
    for k in range(1, chosen_ref.shape[0]):
        hit = hit | (chosen_ref[k:k + 1, :] == sub)
    top = jnp.max(jnp.where(hit, logits, MASK_FILL), axis=0, keepdims=True)
    e = jnp.where(hit, jnp.exp(jnp.where(hit, logits - top, 0.0)), 0.0)
    gates[...] = (e / jnp.sum(e, axis=0, keepdims=True)).T
    out_ref[...] = jnp.zeros_like(out_ref)
    lane = lax.broadcasted_iota(jnp.int32, (rows, experts), 1)
    tile = 256

    def inner(e):
        column = jnp.sum(jnp.where(lane == e, gates[...], 0.0), axis=1, keepdims=True)
        return (column * jax.nn.silu(g_ref[...]) * u_ref[...]).astype(BF16)

    def wide(gate, up):
        g = u = None
        for t in range(0, width, tile):
            hk = h_ref[:, t:t + tile]
            gt = lax.dot_general(hk, gate(t), NT, preferred_element_type=F32)
            ut = lax.dot_general(up(t), hk, NT, preferred_element_type=F32)
            g, u = (gt, ut) if g is None else (g + gt, u + ut)
        return g, u.T

    def narrow(z, down):
        for t in range(0, width, tile):
            out_ref[:, t:t + tile] += jnp.dot(z, down(t), preferred_element_type=F32)

    def views(refs, index):
        return [lambda t, ref=ref: ref[index, :, t:t + tile] for ref in refs]

    def clear():
        g_ref[...] = jnp.zeros_like(g_ref)
        u_ref[...] = jnp.zeros_like(u_ref)

    def step_held(i, carry):
        before = list_ref[0, jnp.maximum(i - 1, 0)]
        z = inner(before)
        g, u = wide(*views((held_g, held_u), list_ref[0, i]))
        narrow(z, *views((held_d,), before))
        g_ref[...], u_ref[...] = g, u
        return carry

    def step_rest(i, carry):
        @pl.when(i + RING - 2 < rest)
        def _():
            fetch(i + RING - 2, True)

        @pl.when(i < rest)
        def _():
            fetch(i, False)

        z = inner(list_ref[0, jnp.maximum(held + i - 1, 0)])
        g, u = wide(*views((ring_g, ring_u), lax.rem(i, RING)))
        narrow(z, *views((ring_d,), lax.rem(i + RING - 1, RING)))
        g_ref[...], u_ref[...] = g, u
        return carry

    clear()

    @pl.when(held > 0)
    def _():
        lax.fori_loop(0, held, step_held, 0)
        before = list_ref[0, held - 1]
        narrow(inner(before), *views((held_d,), before))
        clear()

    @pl.when(rest > 0)
    def _():
        ring_d[RING - 1] = jnp.zeros(ring_d.shape[1:], BF16)
        lax.fori_loop(0, rest + 1, step_rest, 0)


def experts_part(ids, x1, chosen_t, gain, wr_t, held, gate_t, up_t, down):
    rows, width = x1.shape
    n_experts, hidden = gate_t.shape[:2]
    return pl.pallas_call(
        experts_kernel,
        name="experts",
        out_shape=jax.ShapeDtypeStruct((rows, width), F32),
        in_specs=[SMEM, VMEM, VMEM, VMEM, VMEM, VMEM, VMEM, VMEM, ANY, ANY, ANY],
        out_specs=VMEM,
        scratch_shapes=[
            pltpu.VMEM((rows, n_experts), F32), pltpu.VMEM((rows, width), BF16),
            pltpu.VMEM((rows, hidden), F32), pltpu.VMEM((rows, hidden), F32),
            pltpu.VMEM((RING, hidden, width), BF16), pltpu.VMEM((RING, hidden, width), BF16), pltpu.VMEM((RING, hidden, width), BF16),
            pltpu.SemaphoreType.DMA((3, RING)),
        ],
        compiler_params=pltpu.CompilerParams(vmem_limit_bytes=20 * 1024 * 1024),
    )(ids, x1, chosen_t, gain, wr_t, *held, gate_t, up_t, down)


def solution(mesh):
    n = mesh.shape["tp"]
    cache_spec = P("dp", None, "tp", None)
    in_specs = (P("dp", None), cache_spec, cache_spec, P("dp"), P("dp", None), P(None), P(None, "tp"), P(None, "tp"), P(None, "tp"), P("tp", None), P(None), P(None, None), P(None, None, "tp"), P(None, None, "tp"), P(None, "tp", None))
    out_specs = (P("dp", None), cache_spec, cache_spec)
    freq = (np.float32(ROPE_THETA) ** (-np.arange(0, 128, 2, dtype=np.float32) / np.float32(128))).astype(np.float32)
    freq = np.concatenate([freq, freq])[None, :]

    def layer_shard(hidden_in, k_cache, v_cache, seq_lens, chosen, g_attn, w_q, w_k, w_v, w_o, g_moe, w_router, w_gate, w_up, w_down):
        rows, slots, heads, dim = k_cache.shape
        width = hidden_in.shape[1]
        chosen_t = chosen.T
        flat = (rows, slots * heads, dim)
        part, ids, k_next, v_next = attention(
            hidden_in, seq_lens, chosen_t, g_attn.reshape(width // 128, 128), jnp.asarray(freq), w_q, w_k, w_v, w_o,
            k_cache.reshape(flat), v_cache.reshape(flat))
        experts = (jnp.swapaxes(w_gate, 1, 2), jnp.swapaxes(w_up, 1, 2), w_down)
        x1, *held = add_sum(part, hidden_in, n, 1, experts)
        moe = experts_part(ids, x1, chosen_t, g_moe.reshape(width // 128, 128), w_router.T, held, *experts)
        out, = add_sum(moe, x1, n, 2)
        return out, k_next.reshape(k_cache.shape), v_next.reshape(v_cache.shape)

    return jax.shard_map(layer_shard, mesh=mesh, in_specs=in_specs, out_specs=out_specs, check_vma=False)
```

profile of v0, /device:TPU:0, one launch (start us, length us, event | category | flops | bytes accessed | tf_op | source)
XLA Modules:
  0.0 62.5 jit_solution(13955271413523159029)
XLA Ops:
  0.6 0.0 copy-start
  0.6 9.6 %attention.1 = (f32[32,2048]{1,0:T(8,128)}, s32[1,128]{1,0:T(1,128)}, bf16[32,512,128]{2,1,0:T(8,128)(2,1)}, bf16[32,512,128]{2,1,0:T(8,128)(2,1)}) custom-call(bf16[32,2048]{1,0:T(8,128)(2,1)} %base_ref.1, s32[32]{0:T(128)} %lens_ref.1, s32[6,32]{1,0:T(8,128)} %bitcast.11, bf16[16,128]{1,0:T(8,128)(2,1)} %bitcast.20, f32[1,128]{1,0:T(1,128)} %constant.2.clone.freq_ref, ...), custom_call_target="tpu_custom_call" | custom-call | tf_op jit(solution)/shard_map/attention/pallas_call | solution.py:159
  10.2 0.0 copy-done
  10.2 0.0 copy-start.2
  10.2 0.9 %copy-done.2 = f32[32,2048]{1,0:T(8,128)S(1)} copy-done((f32[32,2048]{1,0:T(8,128)S(1)}, f32[32,2048]{1,0:T(8,128)}, u32[]{:S(2)}) %copy-start.2) | copy-done | bytes 262168
  11.2 0.0 copy-start.1
  11.2 0.0 copy-start.3
  11.2 0.0 copy-start.4
  11.2 0.0 copy-start.5
  11.2 13.0 %add_sum.2 = (bf16[32,2048]{1,0:T(8,128)(2,1)S(1)}, bf16[12,176,2048]{2,1,0:T(8,128)(2,1)S(1)}, bf16[12,176,2048]{2,1,0:T(8,128)(2,1)S(1)}, bf16[12,176,2048]{2,1,0:T(8,128)(2,1)S(1)}) custom-call(f32[32,2048]{1,0:T(8,128)S(1)} %copy-done.2, bf16[32,2048]{1,0:T(8,128)(2,1)S(1)} %copy-done, bf16[64,176,2048]{2,1,0:T(8,128)(2,1)} %bitcast.14, ...), custom_call_target="tpu_custom_call" | custom-call | tf_op jit(solution)/shard_map/add_sum/pallas_call | solution.py:234
  24.2 0.0 copy-done.1
  24.2 0.0 copy-done.3
  24.2 0.0 copy-done.4
  24.2 0.0 copy-done.5
  24.2 27.6 %experts.1.part_ref = f32[32,2048]{1,0:T(8,128)S(1)} custom-call(s32[1,128]{1,0:T(1,128)S(1)} %copy-done.5, bf16[32,2048]{1,0:T(8,128)(2,1)S(1)} %get-tuple-element.13.x_ref.base_ref, s32[6,32]{1,0:T(8,128)S(1)} %bitcast.12, bf16[16,128]{1,0:T(8,128)(2,1)S(1)} %bitcast.13, bf16[64,2048]{1,0:T(8,128)(2,1)S(1)} %bitcast.10, ...), custom_call_target="tpu_custom_call" | custom-call | tf_op jit(solution)/shard_map/experts/pallas_call | solution.py:350
  51.8 10.0 %add_sum.3 = bf16[32,2048]{1,0:T(8,128)(2,1)S(1)} custom-call(f32[32,2048]{1,0:T(8,128)S(1)} %experts.1.part_ref, bf16[32,2048]{1,0:T(8,128)(2,1)S(1)} %get-tuple-element.13.x_ref.base_ref), custom_call_target="tpu_custom_call" | custom-call | tf_op jit(solution)/shard_map/add_sum/pallas_call | solution.py:234
  61.8 0.7 %copy.20 = bf16[32,2048]{1,0:T(8,128)(2,1)} copy(bf16[32,2048]{1,0:T(8,128)(2,1)S(1)} %add_sum.3) | data formatting | bytes 262144
Async XLA Ops:
  0.6 9.6 %copy-start = (bf16[32,2048]{1,0:T(8,128)(2,1)S(1)}, bf16[32,2048]{1,0:T(8,128)(2,1)}, u32[]{:S(2)}) copy-start(bf16[32,2048]{1,0:T(8,128)(2,1)} %base_ref.1) | copy-start | bytes 393220
  10.2 1.0 %copy-start.2 = (f32[32,2048]{1,0:T(8,128)S(1)}, f32[32,2048]{1,0:T(8,128)}, u32[]{:S(2)}) copy-start(f32[32,2048]{1,0:T(8,128)} %get-tuple-element.12.part_ref) | copy-start | bytes 786436
  11.2 13.0 %copy-start.1 = (bf16[2048,64]{0,1:T(8,128)(2,1)S(1)}, bf16[2048,64]{0,1:T(8,128)(2,1)}, u32[]{:S(2)}) copy-start(bf16[2048,64]{0,1:T(8,128)(2,1)} %param.27) | copy-start | bytes 786436
  11.2 13.0 %copy-start.3 = (s32[32,6]{0,1:T(8,128)S(1)}, s32[32,6]{0,1:T(8,128)}, u32[]{:S(2)}) copy-start(s32[32,6]{0,1:T(8,128)} %param.20) | copy-start | bytes 2308
  11.2 13.0 %copy-start.4 = (bf16[2048]{0:T(1024)(128)(2,1)S(1)}, bf16[2048]{0:T(1024)(128)(2,1)}, u32[]{:S(2)}) copy-start(bf16[2048]{0:T(1024)(128)(2,1)} %param.26) | copy-start | bytes 12292
  11.2 13.0 %copy-start.5 = (s32[1,128]{1,0:T(1,128)S(1)}, s32[1,128]{1,0:T(1,128)}, u32[]{:S(2)}) copy-start(s32[1,128]{1,0:T(1,128)} %get-tuple-element.11.list_ref) | copy-start | bytes 1540
where the time goes:
time: 61.5 us; the launch traced here: 62.5 us
  Pallas kernels  60.1 us (98%)
  local copies, waits for them, and re-layouts  1.62 us (3%)
  between operations  0.72 us (1%)
    pallas_call x1, Pallas kernels, experts_part(): pl.pallas_call(experts_kernel, name='experts', out_shape=jax.ShapeDtypeSt...  27.6 us
    pallas_call x2, Pallas kernels, add_sum(): pl.pallas_call(functools.partial(sum_kernel, n, len(ahead)), name='add_su...  23 us
    pallas_call x1, Pallas kernels, attention(): pl.pallas_call(attention_kernel, name='attention', out_shape=(jax.ShapeDt...  9.57 us
    unnamed x13, local copies, waits for them, and re-layouts  1.62 us

commit v1 on v0

--- a/solution.py
+++ b/solution.py
@@ -18,9 +18,14 @@
 SMEM = pl.BlockSpec(memory_space=pltpu.SMEM)
 NT = (((1,), (1,)), ((), ()))
 
+
+def in_hbm(*arrays):
+    return [pltpu.with_memory_space_constraint(a, pltpu.HBM) for a in arrays]
+
+
 GROUP = 8
-RING = 8
-HELD = 12
+RING = 5
+HELD = 16
 
 
 def norm_rows(x, gain):
@@ -31,9 +36,10 @@
     return (x32 * scale * gain_row).astype(BF16)
 
 
-def attention_kernel(x_ref, lens_ref, chosen_ref, gain_ref, freq_ref, wq_hbm, wk_hbm, wv_hbm, wo_hbm, k_hbm, v_hbm,
-                     part_ref, list_ref, ko_hbm, vo_hbm,
-                     wq, wk, wv, wo, kbuf, vbuf, qs, ks, vs, os, wsem, ksem, vsem, kosem, vosem):
+def attention_kernel(x_hbm, lens_hbm, chosen_hbm, gain_hbm, freq_hbm, wq_hbm, wk_hbm, wv_hbm, k_hbm, v_hbm,
+                     heads_ref, list_ref, ko_hbm, vo_hbm,
+                     x_ref, lens_ref, chosen_ref, gain_ref, freq_ref, wq, wk, wv, kbuf, vbuf, qs, ks, vs, os,
+                     wsem, ksem, vsem, kosem, vosem):
     rows, width = x_ref.shape
     slots2, dim = kbuf.shape[1], kbuf.shape[2]
     steps = rows // GROUP
@@ -45,13 +51,17 @@
         block = pl.ds(c * GROUP, GROUP)
         return pltpu.make_async_copy(hbm.at[block], buf.at[block], sem.at[c])
 
-    weights = [load(wq_hbm, wq, wsem.at[0]), load(wk_hbm, wk, wsem.at[1]), load(wv_hbm, wv, wsem.at[2]), load(wo_hbm, wo, wsem.at[3])]
-    for copy in weights[:3]:
+    pairs = ((x_hbm, x_ref), (gain_hbm, gain_ref), (lens_hbm, lens_ref), (freq_hbm, freq_ref), (chosen_hbm, chosen_ref),
+             (wq_hbm, wq), (wk_hbm, wk), (wv_hbm, wv))
+    loads = [load(hbm, buf, wsem.at[i]) for i, (hbm, buf) in enumerate(pairs)]
+    weights = loads[5:]
+    for copy in loads:
         copy.start()
     for c in range(steps):
         part(k_hbm, kbuf, ksem, c).start()
         part(v_hbm, vbuf, vsem, c).start()
-    weights[3].start()
+    for copy in loads[:5]:
+        copy.wait()
 
     experts = 64
     sub = lax.broadcasted_iota(jnp.int32, (experts, rows), 0)
@@ -144,106 +154,119 @@
         part(kbuf, ko_hbm, kosem, c).start()
         part(vbuf, vo_hbm, vosem, c).start()
 
-    heads = jnp.concatenate([os[pl.ds(0, rows, stride=2), :], os[pl.ds(1, rows, stride=2), :]], axis=1).astype(BF16)
-    weights[3].wait()
-    for j in range(0, width, 256):
-        part_ref[:, j:j + 256] = jnp.dot(heads, wo[:, j:j + 256], preferred_element_type=F32)
+    heads_ref[...] = jnp.concatenate([os[pl.ds(0, rows, stride=2), :], os[pl.ds(1, rows, stride=2), :]], axis=1).astype(BF16)
     for c in range(steps):
         part(kbuf, ko_hbm, kosem, c).wait()
         part(vbuf, vo_hbm, vosem, c).wait()
 
 
-def attention(x, lens, chosen_t, gain, freq, wq, wk, wv, wo, k_cache, v_cache):
+def attention(x, lens, chosen_t, gain, freq, wq, wk, wv, k_cache, v_cache):
     rows, width = x.shape
     steps = rows // GROUP
     return pl.pallas_call(
         attention_kernel,
         name="attention",
         out_shape=(
-            jax.ShapeDtypeStruct((rows, width), F32),
-            jax.ShapeDtypeStruct((1, 128), jnp.int32),
+            pltpu.VMEM((rows, 256), BF16),
+            pltpu.VMEM((1, 128), jnp.int32),
             jax.ShapeDtypeStruct(k_cache.shape, BF16),
             jax.ShapeDtypeStruct(v_cache.shape, BF16),
         ),
-        in_specs=[VMEM, SMEM, VMEM, VMEM, VMEM] + [ANY] * 6,
+        in_specs=[ANY] * 10,
         out_specs=(VMEM, VMEM, ANY, ANY),
         scratch_shapes=[
-            pltpu.VMEM(wq.shape, BF16), pltpu.VMEM(wk.shape, BF16), pltpu.VMEM(wv.shape, BF16), pltpu.VMEM(wo.shape, BF16),
+            pltpu.VMEM(x.shape, BF16), pltpu.SMEM(lens.shape, jnp.int32), pltpu.VMEM(chosen_t.shape, jnp.int32),
+            pltpu.VMEM(gain.shape, BF16), pltpu.VMEM(freq.shape, F32),
+            pltpu.VMEM(wq.shape, BF16), pltpu.VMEM(wk.shape, BF16), pltpu.VMEM(wv.shape, BF16),
             pltpu.VMEM(k_cache.shape, BF16), pltpu.VMEM(v_cache.shape, BF16),
             pltpu.VMEM((rows, 256), F32), pltpu.VMEM((rows, 256), F32), pltpu.VMEM((rows, 256), F32),
             pltpu.VMEM((2 * rows, 128), F32),
-            pltpu.SemaphoreType.DMA((4,)),
+            pltpu.SemaphoreType.DMA((8,)),
             pltpu.SemaphoreType.DMA((steps,)), pltpu.SemaphoreType.DMA((steps,)),
             pltpu.SemaphoreType.DMA((steps,)), pltpu.SemaphoreType.DMA((steps,)),
         ],
-        compiler_params=pltpu.CompilerParams(vmem_limit_bytes=62 * 1024 * 1024),
-    )(x, lens, chosen_t, gain, freq, wq, wk, wv, wo, k_cache, v_cache)
-
-
-def sum_kernel(n, n_ahead, part_ref, base_ref, *refs):
-    ahead_hbm, (out_ref, *ahead), (inbox, piece, send1, recv1, send2, recv2, *sems) = (
-        refs[:n_ahead], refs[n_ahead:2 * n_ahead + 1], refs[2 * n_ahead + 1:])
+        compiler_params=pltpu.CompilerParams(vmem_limit_bytes=16 * 1024 * 1024),
+    )(*in_hbm(x, lens, chosen_t, gain, freq, wq, wk, wv, k_cache, v_cache))
+
+
+ORDER = (6, 2, 4, 7, 3, 5, 1)
+
+
+def sum_kernel(n_ahead, project, *refs):
+    if project:
+        heads_ref, wo_hbm, *refs = refs
+    else:
+        part_ref, *refs = refs
+    base_ref, *refs = refs
+    ahead_hbm, (out_ref, *ahead), (inbox, piece, sems, *refs) = refs[:n_ahead], refs[n_ahead:2 * n_ahead + 1], refs[2 * n_ahead + 1:]
     me = lax.axis_index("tp")
-    loads = [pltpu.make_async_copy(src.at[pl.ds(e, 2)], dst.at[pl.ds(e, 2)], sems[0].at[m, e // 2])
-             for e in range(0, HELD, 2) for m, (src, dst) in enumerate(zip(ahead_hbm, ahead))]
-    for load in loads:
-        load.start()
-    cols = part_ref.shape[1] // n
-    barrier = pltpu.get_barrier_semaphore()
-    for d in range(1, n):
-        pl.semaphore_signal(barrier, inc=1, device_id={"tp": lax.rem(me + d, n)}, device_id_type=pl.DeviceIdType.MESH)
-    pl.semaphore_wait(barrier, n - 1)
+    core, xx, yy = lax.rem(me, 2), lax.rem(me // 2, 2), me // 4
+    cols = base_ref.shape[1] // 8
+
+    def peer(m):
+        return (1 - yy if m & 4 else yy) * 4 + (1 - xx if m & 2 else xx) * 2 + (1 - core if m & 1 else core)
 
     def columns(j):
         return pl.ds(pl.multiple_of(j * cols, cols), cols)
 
-    first = []
-    for d in range(1, n):
-        to = lax.rem(me + d, n)
-        copy = pltpu.make_async_remote_copy(
-            src_ref=part_ref.at[:, columns(to)], dst_ref=inbox.at[d - 1],
-            send_sem=send1.at[d - 1], recv_sem=recv1.at[d - 1],
-            device_id={"tp": to}, device_id_type=pl.DeviceIdType.MESH)
+    def send(src, dst, m, phase):
+        return pltpu.make_async_remote_copy(
+            src_ref=src, dst_ref=dst, send_sem=sems.at[phase, m], recv_sem=sems.at[phase + 1, m],
+            device_id={"tp": peer(m)}, device_id_type=pl.DeviceIdType.MESH)
+
+    barrier = pltpu.get_barrier_semaphore()
+    for m in ORDER:
+        pl.semaphore_signal(barrier, inc=1, device_id={"tp": peer(m)}, device_id_type=pl.DeviceIdType.MESH)
+    loads = []
+    if project:
+        wo, part_ref, load_sems = refs
+        load_wo = pltpu.make_async_copy(wo_hbm, wo, sems.at[0, 0])
+        load_wo.start()
+        loads = [pltpu.make_async_copy(src.at[pl.ds(e, 2)], dst.at[pl.ds(e, 2)], load_sems.at[m, e // 2])
+                 for e in range(0, HELD, 2) for m, (src, dst) in enumerate(zip(ahead_hbm, ahead))]
+        for load in loads:
+            load.start()
+        load_wo.wait()
+        for j in range(0, base_ref.shape[1], cols):
+            part_ref[:, j:j + cols] = jnp.dot(heads_ref[...], wo[:, j:j + cols], preferred_element_type=F32)
+    pl.semaphore_wait(barrier, len(ORDER))
+
+    first = {m: send(part_ref.at[:, columns(peer(m))], inbox.at[m - 1], m, 0) for m in ORDER}
+    for m in ORDER:
+        first[m].start()
+    total = part_ref[:, columns(me)]
+    for m in (1, 2, 4, 3, 5, 6, 7):
+        first[m].wait_recv()
+        total = total + inbox[m - 1]
+    piece[...] = (base_ref[:, columns(me)].astype(F32) + total).astype(BF16)
+    second = [send(piece, out_ref.at[:, columns(me)], m, 2) for m in ORDER]
+    for copy in second:
         copy.start()
-        first.append(copy)
-    total = part_ref[:, columns(me)]
-    for d in range(1, n):
-        first[d - 1].wait_recv()
-        total = total + inbox[d - 1]
-    piece[...] = (base_ref[:, columns(me)].astype(F32) + total).astype(BF16)
-    second = []
-    for d in range(1, n):
-        to = lax.rem(me + d, n)
-        copy = pltpu.make_async_remote_copy(
-            src_ref=piece, dst_ref=out_ref.at[:, columns(me)],
-            send_sem=send2.at[d - 1], recv_sem=recv2.at[d - 1],
-            device_id={"tp": to}, device_id_type=pl.DeviceIdType.MESH)
-        copy.start()
-        second.append(copy)
     out_ref[:, columns(me)] = piece[...]
-    for d in range(1, n):
-        first[d - 1].wait_send()
-    for d in range(1, n):
-        second[d - 1].wait()
+    for m in ORDER:
+        first[m].wait_send()
+    for copy in second:
+        copy.wait()
     for load in loads:
         load.wait()
 
 
-def add_sum(part, base, n, collective_id, ahead=()):
+def add_sum(partial, base, collective_id, ahead=()):
     rows, width = base.shape
+    project = len(partial) == 2
+    scratch = [pltpu.VMEM((7, rows, width // 8), F32), pltpu.VMEM((rows, width // 8), BF16), pltpu.SemaphoreType.DMA((4, 8))]
+    if project:
+        partial = (partial[0], *in_hbm(partial[1]))
+        scratch += [pltpu.VMEM(partial[1].shape, BF16), pltpu.VMEM((rows, width), F32), pltpu.SemaphoreType.DMA((3, HELD // 2))]
     return pl.pallas_call(
-        functools.partial(sum_kernel, n, len(ahead)),
+        functools.partial(sum_kernel, len(ahead), project),
         name="add_sum",
-        out_shape=[jax.ShapeDtypeStruct(base.shape, BF16)] + [pltpu.VMEM((HELD, *a.shape[1:]), a.dtype) for a in ahead],
-        in_specs=[VMEM, VMEM] + [ANY] * len(ahead),
+        out_shape=[pltpu.VMEM(base.shape, BF16)] + [pltpu.VMEM((HELD, *a.shape[1:]), a.dtype) for a in ahead],
+        in_specs=[VMEM] + [ANY] * (len(partial) - 1) + [VMEM] + [ANY] * len(ahead),
         out_specs=[VMEM] * (1 + len(ahead)),
-        scratch_shapes=[
-            pltpu.VMEM((n - 1, rows, width // n), F32), pltpu.VMEM((rows, width // n), BF16),
-            pltpu.SemaphoreType.DMA((n - 1,)), pltpu.SemaphoreType.DMA((n - 1,)),
-            pltpu.SemaphoreType.DMA((n - 1,)), pltpu.SemaphoreType.DMA((n - 1,)),
-        ] + ([pltpu.SemaphoreType.DMA((len(ahead), HELD // 2))] if ahead else []),
-        compiler_params=pltpu.CompilerParams(collective_id=collective_id, has_side_effects=True, vmem_limit_bytes=8 * 1024 * 1024),
-    )(part, base, *ahead)
+        scratch_shapes=scratch,
+        compiler_params=pltpu.CompilerParams(collective_id=collective_id, has_side_effects=True, vmem_limit_bytes=4 * 1024 * 1024),
+    )(*partial, base, *in_hbm(*ahead))
 
 
 def experts_kernel(list_ref, x_ref, chosen_ref, gain_ref, wr_ref, held_g, held_u, held_d, gate_hbm, up_hbm, down_hbm, out_ref,
@@ -350,7 +373,7 @@
     return pl.pallas_call(
         experts_kernel,
         name="experts",
-        out_shape=jax.ShapeDtypeStruct((rows, width), F32),
+        out_shape=pltpu.VMEM((rows, width), F32),
         in_specs=[SMEM, VMEM, VMEM, VMEM, VMEM, VMEM, VMEM, VMEM, ANY, ANY, ANY],
         out_specs=VMEM,
         scratch_shapes=[
@@ -359,12 +382,11 @@
             pltpu.VMEM((RING, hidden, width), BF16), pltpu.VMEM((RING, hidden, width), BF16), pltpu.VMEM((RING, hidden, width), BF16),
             pltpu.SemaphoreType.DMA((3, RING)),
         ],
-        compiler_params=pltpu.CompilerParams(vmem_limit_bytes=20 * 1024 * 1024),
-    )(ids, x1, chosen_t, gain, wr_t, *held, gate_t, up_t, down)
+        compiler_params=pltpu.CompilerParams(vmem_limit_bytes=12 * 1024 * 1024),
+    )(ids, x1, chosen_t, gain, wr_t, *held, *in_hbm(gate_t, up_t, down))
 
 
 def solution(mesh):
-    n = mesh.shape["tp"]
     cache_spec = P("dp", None, "tp", None)
     in_specs = (P("dp", None), cache_spec, cache_spec, P("dp"), P("dp", None), P(None), P(None, "tp"), P(None, "tp"), P(None, "tp"), P("tp", None), P(None), P(None, None), P(None, None, "tp"), P(None, None, "tp"), P(None, "tp", None))
     out_specs = (P("dp", None), cache_spec, cache_spec)
@@ -372,17 +394,17 @@
     freq = np.concatenate([freq, freq])[None, :]
 
     def layer_shard(hidden_in, k_cache, v_cache, seq_lens, chosen, g_attn, w_q, w_k, w_v, w_o, g_moe, w_router, w_gate, w_up, w_down):
-        rows, slots, heads, dim = k_cache.shape
+        rows, slots, kv_heads, dim = k_cache.shape
         width = hidden_in.shape[1]
         chosen_t = chosen.T
-        flat = (rows, slots * heads, dim)
-        part, ids, k_next, v_next = attention(
-            hidden_in, seq_lens, chosen_t, g_attn.reshape(width // 128, 128), jnp.asarray(freq), w_q, w_k, w_v, w_o,
+        flat = (rows, slots * kv_heads, dim)
+        heads, ids, k_next, v_next = attention(
+            hidden_in, seq_lens, chosen_t, g_attn.reshape(width // 128, 128), jnp.asarray(freq), w_q, w_k, w_v,
             k_cache.reshape(flat), v_cache.reshape(flat))
         experts = (jnp.swapaxes(w_gate, 1, 2), jnp.swapaxes(w_up, 1, 2), w_down)
-        x1, *held = add_sum(part, hidden_in, n, 1, experts)
+        x1, *held = add_sum((heads, w_o), hidden_in, 1, experts)
         moe = experts_part(ids, x1, chosen_t, g_moe.reshape(width // 128, 128), w_router.T, held, *experts)
-        out, = add_sum(moe, x1, n, 2)
+        out, = add_sum((moe,), x1, 2)
         return out, k_next.reshape(k_cache.shape), v_next.reshape(v_cache.shape)
 
     return jax.shard_map(layer_shard, mesh=mesh, in_specs=in_specs, out_specs=out_specs, check_vma=False)

time: 61.5 us -> 70.2 us (1.14); the launches traced: 62.5 us -> 70.1 us
  Pallas kernels: 60.1 us -> 68.7 us
  local copies, waits for them, and re-layouts: 1.62 us -> 0.68 us
    pallas_call x4, Pallas kernels: 60.1 us -> 68.7 us  [the longest x2 32.1 us: add_sum(): pl.pallas_call(functools.partial(sum_kernel, len(ahead), project), name='...]
    unnamed x13 -> x9, local copies, waits for them, and re-layouts: 1.62 us -> 0.68 us
where the time goes in v1:
time: 70.2 us; the launch traced here: 70.1 us
  Pallas kernels  68.7 us (98%)
  between operations  0.73 us (1%)
    pallas_call x2, Pallas kernels, add_sum(): pl.pallas_call(functools.partial(sum_kernel, len(ahead), project), name='...  32.1 us
    pallas_call x1, Pallas kernels, experts_part(): pl.pallas_call(experts_kernel, name='experts', out_shape=pltpu.VMEM((rows...  27.8 us
    pallas_call x1, Pallas kernels, attention(): pl.pallas_call(attention_kernel, name='attention', out_shape=(pltpu.VMEM(...  8.81 us

profile of v1, /device:TPU:0, one launch (start us, length us, event | category | flops | bytes accessed | tf_op | source)
XLA Modules:
  0.0 70.1 jit_solution(9471597091219378138)
XLA Ops:
  0.6 0.0 copy-start
  0.6 8.8 %attention.1 = (bf16[32,256]{1,0:T(8,128)(2,1)S(1)}, s32[1,128]{1,0:T(1,128)S(1)}, bf16[32,512,128]{2,1,0:T(8,128)(2,1)}, bf16[32,512,128]{2,1,0:T(8,128)(2,1)}) custom-call(bf16[32,2048]{1,0:T(8,128)(2,1)} %refs_2_.1, s32[32]{0:T(128)} %lens_hbm.1, s32[6,32]{1,0:T(8,128)} %bitcast.11, bf16[16,128]{1,0:T(8,128)(2,1)} %bitcast.20, ...), custom_call_target="tpu_custom_call" | custom-call | tf_op jit(solution)/shard_map/attention/pallas_call | solution.py:166
  9.5 0.0 copy-done
  9.5 0.0 copy-start.1
  9.5 0.0 copy-start.2
  9.5 0.0 copy-start.3
  9.5 22.1 %add_sum.2 = (bf16[32,2048]{1,0:T(8,128)(2,1)S(1)}, bf16[16,176,2048]{2,1,0:T(8,128)(2,1)S(1)}, bf16[16,176,2048]{2,1,0:T(8,128)(2,1)S(1)}, bf16[16,176,2048]{2,1,0:T(8,128)(2,1)S(1)}) custom-call(bf16[32,256]{1,0:T(8,128)(2,1)S(1)} %get-tuple-element.12.refs_0_, bf16[256,2048]{1,0:T(8,128)(2,1)} %refs_1_.1, bf16[32,2048]{1,0:T(8,128)(2,1)S(1)} %copy-done, ...), custom_call_target="tpu_custom_call" | custom-call | tf_op jit(solution)/shard_map/add_sum/pallas_call | solution.py:261
  31.6 0.0 copy-done.1
  31.7 0.0 copy-done.2
  31.7 0.0 copy-done.3
  31.7 27.8 %experts.1.refs_0_ = f32[32,2048]{1,0:T(8,128)S(1)} custom-call(s32[1,128]{1,0:T(1,128)S(1)} %get-tuple-element.11.list_ref, bf16[32,2048]{1,0:T(8,128)(2,1)S(1)} %get-tuple-element.13.x_ref.refs_1_, s32[6,32]{1,0:T(8,128)S(1)} %bitcast.12, bf16[16,128]{1,0:T(8,128)(2,1)S(1)} %bitcast.13, bf16[64,2048]{1,0:T(8,128)(2,1)S(1)} %bitcast.10, ...), custom_call_target="tpu_custom_call" | custom-call | tf_op jit(solution)/shard_map/experts/pallas_call | solution.py:373
  59.5 9.9 %add_sum.3 = bf16[32,2048]{1,0:T(8,128)(2,1)S(1)} custom-call(f32[32,2048]{1,0:T(8,128)S(1)} %experts.1.refs_0_, bf16[32,2048]{1,0:T(8,128)(2,1)S(1)} %get-tuple-element.13.x_ref.refs_1_), custom_call_target="tpu_custom_call" | custom-call | tf_op jit(solution)/shard_map/add_sum/pallas_call | solution.py:261
  69.5 0.7 copy.20
Async XLA Ops:
  0.6 8.8 %copy-start = (bf16[32,2048]{1,0:T(8,128)(2,1)S(1)}, bf16[32,2048]{1,0:T(8,128)(2,1)}, u32[]{:S(2)}) copy-start(bf16[32,2048]{1,0:T(8,128)(2,1)} %refs_2_.1) | copy-start | bytes 393220
  9.5 22.2 %copy-start.1 = (bf16[2048,64]{0,1:T(8,128)(2,1)S(1)}, bf16[2048,64]{0,1:T(8,128)(2,1)}, u32[]{:S(2)}) copy-start(bf16[2048,64]{0,1:T(8,128)(2,1)} %param.27) | copy-start | bytes 786436
  9.5 22.2 %copy-start.2 = (s32[32,6]{0,1:T(8,128)S(1)}, s32[32,6]{0,1:T(8,128)}, u32[]{:S(2)}) copy-start(s32[32,6]{0,1:T(8,128)} %param.20) | copy-start | bytes 2308
  9.5 22.2 %copy-start.3 = (bf16[2048]{0:T(1024)(128)(2,1)S(1)}, bf16[2048]{0:T(1024)(128)(2,1)}, u32[]{:S(2)}) copy-start(bf16[2048]{0:T(1024)(128)(2,1)} %param.26) | copy-start | bytes 12292
